TPU v7x, 32 devices: a whole 2x2x4 slice. The times are simulated.
32 devices in a mesh: grp: 8 (over z, x), row: 4 (over y, core).
Axes of the slice: x: 2, y: 2, z: 4, core: 2. Of those that a mesh axis runs over, the one named last changes fastest.
Arguments:
- gll_state: float32 [8, 32, 16, 4096], P(None, None, None, ('grp', 'row')), may hold values from -6 to 6
- metric: float32 [16, 4096], P(None, ('grp', 'row')), may hold values from 0.7 to 1.4
- phys_owner: int32 [4096, 4, 1], P(('grp', 'row')), may hold values from 0 to 7; in each aligned block of 512 rows (0 to 511, 512 to 1023, ..., all dimensions but the last counted through in order) at most 128 rows name the same one
- neighbours: int32 [4, 4096], P(None, ('grp', 'row')), may hold values from 0 to 4095, as said below
- phys_rate: float32 [32, 32768], P(None, ('grp', 'row')), may hold values from 0.2 to 2
- phys_forcing: float32 [32, 32768], P(None, ('grp', 'row')), may hold values from -6 to 6
- field_mix: float32 [8, 8], replicated, may hold values from -2 to 2
Outputs:
- gll_tend: float32 [8, 32, 16, 4096], P(None, None, None, ('grp', 'row'))
Inputs may be any that keep to these rules, and one draw needn't show every extreme that they name: `phys_owner`: in the 512 rows of one device, no owner is named more than 128 times, and some owner reaches 128. `neighbours`: rows 0 and 1 of element e are e - 1 and e + 1, cyclically over 4096 elements; rows 2 and 3 lie 2 to 32 positions before and after e, cyclically, and some element has a neighbour exactly 32 positions away.
All inputs are finite; a program needn't handle non-finite values.
Results may differ from a plain program's by a relative error of at most 0.000094.
Values sent between devices are 32-bit elements; how exact they have to be, the bound alone decides.
A program may use at most 64 MiB of HBM per device.

v0:
```python
import functools

import jax
import jax.numpy as jnp
import numpy as np
from jax import lax
from jax.experimental import pallas as pl
from jax.experimental.pallas import tpu as pltpu
from jax.sharding import PartitionSpec as P

HALO = 32
MESH = pl.DeviceIdType.MESH
PARTS = 4
LANES = 128
GLL = [-1.0, -1.0 / np.sqrt(5.0), 1.0 / np.sqrt(5.0), 1.0]


def half_weights():
    offset = 0.5 / np.sqrt(3.0)
    halves = np.zeros((2, 4))
    for i in range(4):
        for a, middle in enumerate((-0.5, 0.5)):
            for point in (middle - offset, middle + offset):
                value = 0.5
                for k in range(4):
                    if k != i:
                        value *= (point - GLL[k]) / (GLL[i] - GLL[k])
                halves[a, i] += value
    return halves


def pick(index, values):
    out = jnp.full(index.shape, np.float32(values[-1]), jnp.float32)
    for k in range(len(values) - 1):
        out = jnp.where(index == k, np.float32(values[k]), out)
    return out


def split(x):
    high = x.astype(jnp.bfloat16)
    low = (x - high.astype(jnp.float32)).astype(jnp.bfloat16)
    return high, low


def nodes_writer(row_size, neighbours, fields, elems):
    flat = lax.axis_index("grp") * row_size + lax.axis_index("row")
    inside, places = [], []
    for k in range(4):
        spot = neighbours[k : k + 1] - flat * elems
        within = jnp.where((spot >= 0) & (spot < elems), 1, 0)
        inside.append(jnp.broadcast_to(within, (fields, elems)) == 1)
        places.append(jnp.broadcast_to(neighbours[k : k + 1] % elems, (fields, elems)))
    lane = lax.broadcasted_iota(jnp.int32, (fields, elems), 1)
    sub = lax.broadcasted_iota(jnp.int32, (8, elems), 0)
    gi = pick(sub % 4, GLL)
    gj = [pick(sub // 4, GLL[:2]), pick(sub // 4, GLL[2:])]
    left_x, right_x = 0.5 - gi, 0.5 + gi
    low_y = [0.5 - g for g in gj]
    high_y = [0.5 + g for g in gj]
    slope_left = 0.5 * jnp.maximum(0.0, -gi)
    slope_right = 0.5 * jnp.maximum(0.0, gi)
    slope_y = [0.5 * jnp.maximum(0.0, -gj[0]), 0.5 * jnp.maximum(0.0, gj[1])]

    def take(x, index):
        return jnp.take_along_axis(x, index, axis=1, mode="promise_in_bounds")

    def write(tend_ref, from_left, from_right, p, work_ref, store):
        cells = [tend_ref[pl.ds(c * fields, fields), :] for c in range(4)]
        own = (cells[0] + cells[1] + cells[2] + cells[3]) * np.float32(0.25)
        from_left = pltpu.roll(from_left, (elems - HALO * (p + 1)) % elems, 1)
        if p:
            from_right = pltpu.roll(from_right, elems - HALO * p, 1)
        halo = jnp.where(lane < elems // 2, from_right, from_left)
        around = [
            jnp.where(inside[k], take(own, places[k]), take(halo, places[k])) for k in range(4)
        ]
        low = functools.reduce(jnp.minimum, cells + around)
        high = functools.reduce(jnp.maximum, cells + around)
        for k in range(4):
            work_ref[k] = around[k] - own
        work_ref[4] = low
        work_ref[5] = high
        for f in range(fields):
            cell = [tend_ref[pl.ds(c * fields + f, 1), :] for c in range(4)]
            west, east, south, north, lower, upper = (
                work_ref[k, pl.ds(f, 1), :] for k in range(6)
            )
            bottom = left_x * cell[0] + right_x * cell[1]
            top = left_x * cell[2] + right_x * cell[3]
            slope = slope_left * west + slope_right * east
            for v, side in ((0, south), (1, north)):
                value = low_y[v] * bottom + high_y[v] * top + (slope + slope_y[v] * side)
                store(f, v, jnp.minimum(jnp.maximum(value, lower), upper))

    return write


def exchange_kernel(
    grp_size,
    row_size,
    gll_ref,
    metric_ref,
    owner_ref,
    rate_ref,
    forcing_ref,
    mix_ref,
    neighbours_ref,
    done_ref,
    tail_ref,
    tail_halo_ref,
    gll_v,
    metric_v,
    owner_v,
    mix_v,
    neighbours_v,
    slots_v,
    mixed_v,
    recv_v,
    sel_v,
    tend_v,
    pack_v,
    halo_v,
    work_v,
    gll_sem,
    small_sem,
    slots_sem,
    send_sem,
    recv_sem,
    halo_send_sem,
    halo_recv_sem,
    ready_sem,
    near_sem,
):
    fields, levels, nodes, elems = gll_v.shape
    part = levels // PARTS
    cap = recv_v.shape[3]

    def block_of(peer):
        return pl.ds(pl.multiple_of(peer * cap, cap), cap)

    chunks = gll_sem.shape[0]
    chunk = levels // chunks
    pack = elems // HALO
    packs = part // pack
    me = lax.axis_index("grp")
    row = lax.axis_index("row")
    flat = me * row_size + row
    total = grp_size * row_size
    right = lax.rem(flat + 1, total)
    left = lax.rem(flat + total - 1, total)
    right_id = (right // row_size, lax.rem(right, row_size))
    left_id = (left // row_size, lax.rem(left, row_size))

    barrier = pltpu.get_barrier_semaphore()
    first, last = flat == 0, flat == total - 1

    def greet(when, semaphore, device):
        @pl.when(when)
        def _():
            pl.semaphore_signal(semaphore, inc=1, device_id=device, device_id_type=MESH)

    def hear(when, semaphore):
        @pl.when(when)
        def _():
            pl.semaphore_wait(semaphore, 1)

    for peer in range(1, grp_size):
        greet(peer > me, barrier, (peer, row))
    greet(jnp.logical_not(last), barrier, right_id)
    greet(first, barrier, left_id)

    slot_copies = []
    for h in range(PARTS):
        for kind, ref in enumerate((rate_ref, forcing_ref)):
            copy = pltpu.make_async_copy(
                ref.at[pl.ds(h * part, part)],
                slots_v.at[h, pl.ds(kind * part, part)],
                slots_sem.at[h, kind],
            )
            copy.start()
            slot_copies.append(copy)
    small_copies = []
    for k, (src, dst) in enumerate(
        (
            (owner_ref, owner_v),
            (metric_ref, metric_v),
            (mix_ref, mix_v),
            (neighbours_ref, neighbours_v),
        )
    ):
        copy = pltpu.make_async_copy(src, dst, small_sem.at[k])
        copy.start()
        small_copies.append(copy)
    gll_copies = []
    for k in range(chunks):
        span = pl.ds(k * chunk, chunk)
        copy = pltpu.make_async_copy(gll_ref.at[:, span], gll_v.at[:, span], gll_sem.at[k])
        copy.start()
        gll_copies.append(copy)

    @pl.when(jnp.logical_not(first))
    def _():
        pl.semaphore_wait(barrier, me + jnp.where(last, 2, 1))

    for peer in range(grp_size - 1):
        greet(peer < me, ready_sem.at[me], (peer, row))
    greet(jnp.logical_not(first), near_sem.at[0], left_id)
    greet(last, near_sem.at[1], right_id)

    arrivals = {}
    for h in range(PARTS):
        for i in range(1, grp_size):
            peer = lax.rem(me + i, grp_size)
            arrivals[h, i] = pltpu.make_async_remote_copy(
                src_ref=slots_v.at[h, :, block_of(peer)],
                dst_ref=recv_v.at[h, i - 1],
                send_sem=send_sem,
                recv_sem=recv_sem.at[h],
                device_id=(peer, row),
                device_id_type=MESH,
            )
    for h in range(PARTS):
        for copy in slot_copies[2 * h : 2 * h + 2]:
            copy.wait()
        for i in range(1, grp_size):
            pl.when(me + i >= grp_size)(arrivals[h, i].start)

    def send_later(i):
        @pl.when(me + i < grp_size)
        def _():
            pl.semaphore_wait(ready_sem.at[me + i], 1)
            for h in range(PARTS):
                arrivals[h, i].start()

    for copy in small_copies:
        copy.wait()

    grp_iota = lax.broadcasted_iota(jnp.int32, (grp_size, elems), 0)
    named = [
        jnp.where(owner_v[c] == grp_iota, np.float32(1), np.float32(0)) for c in range(4)
    ]
    before = (
        lax.broadcasted_iota(jnp.int32, (elems, elems), 0)
        < lax.broadcasted_iota(jnp.int32, (elems, elems), 1)
    )
    running = jnp.dot(
        (named[0] + named[1] + named[2] + named[3]).astype(jnp.bfloat16),
        jnp.where(before, np.float32(1), np.float32(0)).astype(jnp.bfloat16),
        preferred_element_type=jnp.float32,
    )
    targets = []
    for c in range(4):
        rank = jnp.sum(named[c] * running, axis=0, keepdims=True).astype(jnp.int32)
        running = running + named[c]
        slot = me - owner_v[c]
        slot = jnp.where(slot < 0, slot + grp_size, slot)
        targets.append(slot * cap + rank)

    blocks = [jnp.broadcast_to(t // LANES, (2 * part, elems)) for t in targets]
    places = [jnp.broadcast_to(t % LANES, (2 * part, elems)) for t in targets]

    halves = half_weights()
    width = fields * nodes
    lane = lax.broadcasted_iota(jnp.int32, (fields, width), 1)
    spread = jnp.where(
        lane // nodes == lax.broadcasted_iota(jnp.int32, (fields, width), 0),
        np.float32(1),
        np.float32(0),
    )
    mix = jnp.dot(
        mix_v[...], spread, precision=lax.Precision.HIGHEST, preferred_element_type=jnp.float32
    )
    node = lane % nodes
    row_node = lax.broadcasted_iota(jnp.int32, (nodes, elems), 0)
    metric = metric_v[...]
    rows, scales = [], []
    for c in range(4):
        a, b = c % 2, c // 2
        rows.append(mix * pick(node % 4, halves[a]) * pick(node // 4, halves[b]))
        weights = pick(row_node % 4, halves[a]) * pick(row_node // 4, halves[b])
        area = jnp.sum(weights * metric, axis=0, keepdims=True)
        scales.append(jnp.broadcast_to(1.0 / area, (fields, elems)))
    scale = jnp.concatenate(scales, axis=0)
    high, low = split(jnp.concatenate(rows, axis=0))
    matrix = jnp.concatenate(
        [
            jnp.concatenate([high, high], axis=1),
            jnp.concatenate([low, jnp.zeros_like(low)], axis=1),
        ],
        axis=0,
    )
    count = 4 * fields

    def weigh(level):
        x = (gll_v[:, level] * metric[None]).reshape(width, elems)
        return jnp.concatenate(split(x), axis=0)

    for k in range(chunks):
        gll_copies[k].wait()

        def remap(j, carry):
            level = k * chunk + 2 * j
            data = jnp.concatenate([weigh(level), weigh(level + 1)], axis=1)
            out = jnp.dot(matrix, data, preferred_element_type=jnp.float32)
            out = out[:count] + out[count:]
            mixed_v[level] = out[:, :elems] * scale
            mixed_v[level + 1] = out[:, elems:] * scale
            return carry

        lax.fori_loop(0, chunk // 2, remap, 0, unroll=True)
        if k + 1 < grp_size:
            send_later(k + 1)

    for i in range(chunks + 1, grp_size):
        send_later(i)

    quarter = lax.broadcasted_iota(jnp.int32, (fields, elems), 1) // HALO
    hear(jnp.logical_not(last), near_sem.at[0])
    hear(first, near_sem.at[1])
    halo_copies = []
    for h in range(PARTS):
        picked = [None] * 4
        whole = recv_v.at[h]
        pltpu.make_async_copy(whole, whole, recv_sem.at[h]).wait()
        for i in range(grp_size):
            if i == 0:
                held = slots_v[h, :, block_of(me)]
            else:
                held = recv_v[h, i - 1]
            for k in range(cap // LANES):
                source = held[:, k * LANES : (k + 1) * LANES]
                for c in range(4):
                    value = jnp.take_along_axis(
                        source, places[c], axis=1, mode="promise_in_bounds"
                    )
                    if picked[c] is None:
                        picked[c] = value
                    else:
                        block = i * (cap // LANES) + k
                        picked[c] = jnp.where(blocks[c] == block, value, picked[c])
        for c in range(4):
            sel_v[h, c] = picked[c]
        for q in range(packs):
            to_right = to_left = None
            for p in range(pack):
                at = q * pack + p
                level = h * part + at
                mean = None
                for c in range(4):
                    span = pl.ds(c * fields, fields)
                    tend = sel_v[h, c, pl.ds(at, 1)] * jnp.tanh(
                        mixed_v[level, span] + sel_v[h, c, pl.ds(part + at, 1)]
                    )
                    if h == PARTS - 1:
                        tail_ref[at, span] = tend
                    else:
                        tend_v[level, span] = tend
                    mean = tend if mean is None else mean + tend
                mean = mean * np.float32(0.25)
                to_r = pltpu.roll(mean, (HALO * (p + 1)) % elems, 1) if (p + 1) % pack else mean
                to_l = pltpu.roll(mean, HALO * p, 1) if p else mean
                to_right = to_r if p == 0 else jnp.where(quarter == p, to_r, to_right)
                to_left = to_l if p == 0 else jnp.where(quarter == p, to_l, to_left)
            pack_v[0, h * packs + q] = to_right
            pack_v[1, h * packs + q] = to_left
        span = pl.ds(h * packs, packs)
        for way, device in ((0, right_id), (1, left_id)):
            copy = pltpu.make_async_remote_copy(
                src_ref=pack_v.at[way, span],
                dst_ref=halo_v.at[way, span],
                send_sem=halo_send_sem.at[h, way],
                recv_sem=halo_recv_sem.at[h, way],
                device_id=device,
                device_id_type=MESH,
            )
            copy.start()
            halo_copies.append(copy)

    pltpu.make_async_copy(recv_v, recv_v, send_sem).wait()
    write = nodes_writer(row_size, neighbours_v[...], fields, elems)
    for h in range(PARTS - 1):
        halo_copies[2 * h].wait()
        halo_copies[2 * h + 1].wait()

        def group(q, carry):
            for p in range(pack):
                level = q * pack + p

                def store(f, v, value):
                    done_ref[f, level, pl.ds(8 * v, 8), :] = value

                write(
                    tend_v.at[level], halo_v[0, q], halo_v[1, q], p, work_v.at[p], store
                )
            return carry

        lax.fori_loop(h * packs, (h + 1) * packs, group, 0)
    for copy in halo_copies[2 * PARTS - 2 :]:
        copy.wait()
    for way in range(2):
        for q in range(packs):
            tail_halo_ref[way, q] = halo_v[way, levels // pack - packs + q]


def last_part_kernel(
    row_size, done_ref, tend_ref, halo_ref, neighbours_ref, out_ref, last_v, work_v, sem
):
    fields, part, nodes, elems = last_v.shape
    pack = elems // HALO
    before = done_ref.shape[1]
    copies = []
    for k in range(before // part):
        span = pl.ds(k * part, part)
        copy = pltpu.make_async_copy(done_ref.at[:, span], out_ref.at[:, span], sem.at[k])
        copy.start()
        copies.append(copy)
    write = nodes_writer(row_size, neighbours_ref[...], fields, elems)
    for q in range(part // pack):
        for p in range(pack):
            level = q * pack + p

            def store(f, v, value):
                last_v[f, level, pl.ds(8 * v, 8), :] = value

            write(
                tend_ref.at[level], halo_ref[0, q], halo_ref[1, q], p, work_v.at[level], store
            )
        copy = pltpu.make_async_copy(
            last_v.at[:, pl.ds(q * pack, pack)],
            out_ref.at[:, pl.ds(before + q * pack, pack)],
            sem.at[before // part + q],
        )
        copy.start()
        copies.append(copy)
    for copy in copies:
        copy.wait()


def on_device(gll_state, metric, phys_owner, neighbours, phys_rate, phys_forcing, field_mix):
    fields, levels, nodes, elems = gll_state.shape
    grp_size = lax.axis_size("grp")
    row_size = lax.axis_size("row")
    capacity = phys_rate.shape[1] // grp_size
    cap = -(-capacity // 128) * 128
    if cap != capacity:
        phys_rate, phys_forcing = (
            jnp.pad(
                x.reshape(levels, grp_size, capacity), ((0, 0), (0, 0), (0, cap - capacity))
            ).reshape(levels, grp_size * cap)
            for x in (phys_rate, phys_forcing)
        )
    owner = phys_owner.transpose(1, 2, 0)
    pack = elems // HALO
    part = levels // PARTS
    chunks = 4
    vmem = pl.BlockSpec(memory_space=pltpu.VMEM)
    hbm = pl.BlockSpec(memory_space=pltpu.HBM)
    before = levels - part
    done, tail, tail_halo = pl.pallas_call(
        functools.partial(exchange_kernel, grp_size, row_size),
        out_shape=(
            jax.ShapeDtypeStruct((fields, before, nodes, elems), jnp.float32),
            jax.ShapeDtypeStruct((part, 4 * fields, elems), jnp.float32),
            jax.ShapeDtypeStruct((2, part // pack, fields, elems), jnp.float32),
        ),
        in_specs=[hbm] * 7,
        out_specs=(vmem, vmem, vmem),
        scratch_shapes=[
            pltpu.VMEM((fields, levels, nodes, elems), jnp.float32),
            pltpu.VMEM((nodes, elems), jnp.float32),
            pltpu.VMEM((4, 1, elems), jnp.int32),
            pltpu.VMEM((fields, fields), jnp.float32),
            pltpu.VMEM((4, elems), jnp.int32),
            pltpu.VMEM((PARTS, 2 * part, grp_size * cap), jnp.float32),
            pltpu.VMEM((levels, 4 * fields, elems), jnp.float32),
            pltpu.VMEM((PARTS, grp_size - 1, 2 * part, cap), jnp.float32),
            pltpu.VMEM((PARTS, 4, 2 * part, elems), jnp.float32),
            pltpu.VMEM((before, 4 * fields, elems), jnp.float32),
            pltpu.VMEM((2, levels // pack, fields, elems), jnp.float32),
            pltpu.VMEM((2, levels // pack, fields, elems), jnp.float32),
            pltpu.VMEM((pack, 6, fields, elems), jnp.float32),
            pltpu.SemaphoreType.DMA((chunks,)),
            pltpu.SemaphoreType.DMA((4,)),
            pltpu.SemaphoreType.DMA((PARTS, 2)),
            pltpu.SemaphoreType.DMA,
            pltpu.SemaphoreType.DMA((PARTS,)),
            pltpu.SemaphoreType.DMA((PARTS, 2)),
            pltpu.SemaphoreType.DMA((PARTS, 2)),
            pltpu.SemaphoreType.REGULAR((grp_size,)),
            pltpu.SemaphoreType.REGULAR((2,)),
        ],
        compiler_params=pltpu.CompilerParams(
            collective_id=0, has_side_effects=True, vmem_limit_bytes=32 * 1024 * 1024
        ),
        name="exchange",
    )(
        *(
            pltpu.with_memory_space_constraint(x, pltpu.HBM)
            for x in (
                gll_state,
                metric,
                owner,
                phys_rate,
                phys_forcing,
                field_mix,
                neighbours,
            )
        )
    )
    anywhere = pl.BlockSpec(memory_space=pl.ANY)
    return pl.pallas_call(
        functools.partial(last_part_kernel, row_size),
        out_shape=jax.ShapeDtypeStruct(gll_state.shape, jnp.float32),
        in_specs=[anywhere, vmem, vmem, vmem],
        out_specs=anywhere,
        scratch_shapes=[
            pltpu.VMEM((fields, part, nodes, elems), jnp.float32),
            pltpu.VMEM((part, 6, fields, elems), jnp.float32),
            pltpu.SemaphoreType.DMA((PARTS - 1 + part // pack,)),
        ],
        compiler_params=pltpu.CompilerParams(vmem_limit_bytes=16 * 1024 * 1024),
        name="last_part",
    )(done, tail, tail_halo, neighbours)


def solution(mesh):
    in_specs = (
        P(None, None, None, ("grp", "row")),
        P(None, ("grp", "row")),
        P(("grp", "row"), None, None),
        P(None, ("grp", "row")),
        P(None, ("grp", "row")),
        P(None, ("grp", "row")),
        P(),
    )
    out_specs = P(None, None, None, ("grp", "row"))
    return jax.shard_map(
        on_device, mesh=mesh, in_specs=in_specs, out_specs=out_specs, check_vma=False
    )
```

profile of v0, /device:TPU:0, one launch (start us, length us, event | category | flops | bytes accessed | tf_op | source)
XLA Modules:
  0.0 19.2 jit_solution(11414282851542869307)
XLA Ops:
  0.0 0.0 copy-start
  0.0 17.7 %exchange.1 = (f32[8,24,16,128]{3,2,1,0:T(8,128)S(1)}, f32[8,32,128]{2,1,0:T(8,128)S(1)}, f32[2,2,8,128]{3,2,1,0:T(8,128)S(1)}) custom-call(f32[8,32,16,128]{3,2,1,0:T(8,128)} %gll_ref.1, f32[16,128]{1,0:T(8,128)} %metric_ref.1, s32[4,1,128]{2,1,0:T(1,128)} %bitcast.1, f32[32,1024]{1,0:T(8,128)} %rate_ref.1, f32[32,1024]{1,0:T(8,128)} %forcing_ref.1, ...), custom_call_target="tpu_custom_call" | custom-call | tf_op jit(solution)/shard_map/exchange/pallas_call | solution.py:459
  17.7 0.0 copy-done
  17.7 1.5 %last_part.1 = f32[8,32,16,128]{3,2,1,0:T(8,128)} custom-call(f32[8,24,16,128]{3,2,1,0:T(8,128)S(1)} %get-tuple-element.8.done_ref, f32[8,32,128]{2,1,0:T(8,128)S(1)} %get-tuple-element.9.tend_ref, f32[2,2,8,128]{3,2,1,0:T(8,128)S(1)} %get-tuple-element.10.halo_ref, s32[4,128]{1,0:T(4,128)S(1)} %copy-done), custom_call_target="tpu_custom_call" | custom-call | tf_op jit(solution)/shard_map/last_part/pallas_call | solution.py:511
Async XLA Ops:
  0.0 17.7 %copy-start = (s32[4,128]{1,0:T(4,128)S(1)}, s32[4,128]{1,0:T(4,128)}, u32[]{:S(2)}) copy-start(s32[4,128]{1,0:T(4,128)} %neighbours_ref.3) | copy-start | bytes 6148
where the time goes:
time: 19.3 us; the launch traced here: 19.2 us
  Pallas kernels  19.2 us (99%)
    pallas_call x1, Pallas kernels, on_device(): pl.pallas_call(functools.partial(exchange_kernel, grp_size, row_size), ou...  17.7 us
    pallas_call x1, Pallas kernels, on_device(): pl.pallas_call(functools.partial(last_part_kernel, row_size), out_shape=j...  1.47 us

commit v1 on v0

--- a/solution.py
+++ b/solution.py
@@ -166,7 +166,8 @@
 
     for peer in range(1, grp_size):
         greet(peer > me, barrier, (peer, row))
-    greet(jnp.logical_not(last), barrier, right_id)
+    for peer in range(1, row_size):
+        greet(peer > row, barrier, (me, peer))
     greet(first, barrier, left_id)
 
     slot_copies = []
@@ -200,11 +201,11 @@
 
     @pl.when(jnp.logical_not(first))
     def _():
-        pl.semaphore_wait(barrier, me + jnp.where(last, 2, 1))
+        pl.semaphore_wait(barrier, me + row + jnp.where(last, 1, 0))
 
     for peer in range(grp_size - 1):
         greet(peer < me, ready_sem.at[me], (peer, row))
-    greet(jnp.logical_not(first), near_sem.at[0], left_id)
+    greet(row > 0, near_sem.at[0], left_id)
     greet(last, near_sem.at[1], right_id)
 
     arrivals = {}
@@ -219,18 +220,41 @@
                 device_id=(peer, row),
                 device_id_type=MESH,
             )
-    for h in range(PARTS):
-        for copy in slot_copies[2 * h : 2 * h + 2]:
-            copy.wait()
-        for i in range(1, grp_size):
-            pl.when(me + i >= grp_size)(arrivals[h, i].start)
+    for copy in slot_copies:
+        copy.wait()
+    for g in range(2):
+        for h in range(PARTS):
+            for i in range(1, grp_size):
+                j = me + i - grp_size
+                ok = jnp.logical_and(j >= 0, (j < grp_size // 4) == (g == 0))
+                pl.when(ok)(arrivals[h, i].start)
 
     def send_later(i):
         @pl.when(me + i < grp_size)
         def _():
             pl.semaphore_wait(ready_sem.at[me + i], 1)
+
+        if i == 1:
+            greet(
+                jnp.logical_and(me < grp_size - 1, row == row_size - 1),
+                near_sem.at[1],
+                right_id,
+            )
+
+        @pl.when(me + i < grp_size - 1)
+        def _():
+            for h in range(PARTS // 2):
+                arrivals[h, i].start()
+
+        @pl.when(me + i == grp_size - 1)
+        def _():
             for h in range(PARTS):
                 arrivals[h, i].start()
+
+    def send_rest():
+        for h in range(PARTS // 2, PARTS):
+            for i in range(1, grp_size):
+                pl.when(me + i < grp_size - 1)(arrivals[h, i].start)
 
     for copy in small_copies:
         copy.wait()
@@ -313,10 +337,11 @@
 
     for i in range(chunks + 1, grp_size):
         send_later(i)
+    send_rest()
 
     quarter = lax.broadcasted_iota(jnp.int32, (fields, elems), 1) // HALO
-    hear(jnp.logical_not(last), near_sem.at[0])
-    hear(first, near_sem.at[1])
+    hear(row < row_size - 1, near_sem.at[0])
+    hear(row == 0, near_sem.at[1])
     halo_copies = []
     for h in range(PARTS):
         picked = [None] * 4

time: 19.3 us -> 17.7 us (0.917)
  Pallas kernels: 19.2 us -> 17.5 us
    pallas_call x1, Pallas kernels: 17.7 us -> 16 us  [on_device(): pl.pallas_call(functools.partial(exchange_kernel, grp_size, row_size), ou...]
where the time goes in v1:
time: 17.7 us; the launch traced here: 17.5 us
  Pallas kernels  17.5 us (99%)
    pallas_call x1, Pallas kernels, on_device(): pl.pallas_call(functools.partial(exchange_kernel, grp_size, row_size), ou...  16 us
    pallas_call x1, Pallas kernels, on_device(): pl.pallas_call(functools.partial(last_part_kernel, row_size), out_shape=j...  1.47 us

profile of v1, /device:TPU:0, one launch (start us, length us, event | category | flops | bytes accessed | tf_op | source)
XLA Modules:
  0.0 17.5 jit_solution(9401996244158007815)
XLA Ops:
  0.0 0.0 copy-start
  0.0 16.0 %exchange.1 = (f32[8,24,16,128]{3,2,1,0:T(8,128)S(1)}, f32[8,32,128]{2,1,0:T(8,128)S(1)}, f32[2,2,8,128]{3,2,1,0:T(8,128)S(1)}) custom-call(f32[8,32,16,128]{3,2,1,0:T(8,128)} %gll_ref.1, f32[16,128]{1,0:T(8,128)} %metric_ref.1, s32[4,1,128]{2,1,0:T(1,128)} %bitcast.1, f32[32,1024]{1,0:T(8,128)} %rate_ref.1, f32[32,1024]{1,0:T(8,128)} %forcing_ref.1, ...), custom_call_target="tpu_custom_call" | custom-call | tf_op jit(solution)/shard_map/exchange/pallas_call | solution.py:484
  16.0 0.0 copy-done
  16.1 1.5 %last_part.1 = f32[8,32,16,128]{3,2,1,0:T(8,128)} custom-call(f32[8,24,16,128]{3,2,1,0:T(8,128)S(1)} %get-tuple-element.8.done_ref, f32[8,32,128]{2,1,0:T(8,128)S(1)} %get-tuple-element.9.tend_ref, f32[2,2,8,128]{3,2,1,0:T(8,128)S(1)} %get-tuple-element.10.halo_ref, s32[4,128]{1,0:T(4,128)S(1)} %copy-done), custom_call_target="tpu_custom_call" | custom-call | tf_op jit(solution)/shard_map/last_part/pallas_call | solution.py:536
Async XLA Ops:
  0.0 16.0 %copy-start = (s32[4,128]{1,0:T(4,128)S(1)}, s32[4,128]{1,0:T(4,128)}, u32[]{:S(2)}) copy-start(s32[4,128]{1,0:T(4,128)} %neighbours_ref.3) | copy-start | bytes 6148

commit v2 on v0

--- a/solution.py
+++ b/solution.py
@@ -130,6 +130,7 @@
     halo_recv_sem,
     ready_sem,
     near_sem,
+    far_sem,
 ):
     fields, levels, nodes, elems = gll_v.shape
     part = levels // PARTS
@@ -164,11 +165,9 @@
         def _():
             pl.semaphore_wait(semaphore, 1)
 
-    for peer in range(1, grp_size):
-        greet(peer > me, barrier, (peer, row))
-    greet(jnp.logical_not(last), barrier, right_id)
-    greet(first, barrier, left_id)
-
+    wide = 2 if grp_size % 2 == 0 else 1
+    deep, side = me // wide, lax.rem(me, wide)
+    even = lax.rem(row, 2) == 0
     slot_copies = []
     for h in range(PARTS):
         for kind, ref in enumerate((rate_ref, forcing_ref)):
@@ -179,6 +178,15 @@
             )
             copy.start()
             slot_copies.append(copy)
+    for peer in range(1, grp_size):
+        greet(
+            jnp.logical_and(peer > me, side <= peer % wide), barrier, (peer, row)
+        )
+    odd = jnp.logical_not(even)
+    greet(odd, barrier, (me, row - 1))
+    greet(jnp.logical_and(odd, row < row_size - 1), barrier, (me, row + 1))
+    greet(row == 1, barrier, (me, row_size - 1))
+
     small_copies = []
     for k, (src, dst) in enumerate(
         (
@@ -198,14 +206,26 @@
         copy.start()
         gll_copies.append(copy)
 
-    @pl.when(jnp.logical_not(first))
+    def count(*conditions):
+        return sum(jnp.where(c, 1, 0) for c in conditions)
+
+    heard = (
+        (deep + 1) * (side + 1)
+        - 1
+        + count(even, jnp.logical_and(even, row > 0), row == row_size - 1)
+    )
+
+    @pl.when(heard > 0)
     def _():
-        pl.semaphore_wait(barrier, me + jnp.where(last, 2, 1))
+        pl.semaphore_wait(barrier, heard)
 
     for peer in range(grp_size - 1):
-        greet(peer < me, ready_sem.at[me], (peer, row))
-    greet(jnp.logical_not(first), near_sem.at[0], left_id)
-    greet(last, near_sem.at[1], right_id)
+        greet(
+            jnp.logical_and(peer < me, peer % wide <= side), ready_sem.at[me], (peer, row)
+        )
+    greet(jnp.logical_and(even, row > 0), near_sem.at[0], (me, row - 1))
+    greet(even, near_sem.at[1], (me, row + 1))
+    greet(row == row_size - 1, far_sem.at[0], (me, 1))
 
     arrivals = {}
     for h in range(PARTS):
@@ -219,18 +239,94 @@
                 device_id=(peer, row),
                 device_id_type=MESH,
             )
-    for h in range(PARTS):
-        for copy in slot_copies[2 * h : 2 * h + 2]:
-            copy.wait()
-        for i in range(1, grp_size):
-            pl.when(me + i >= grp_size)(arrivals[h, i].start)
-
-    def send_later(i):
-        @pl.when(me + i < grp_size)
-        def _():
-            pl.semaphore_wait(ready_sem.at[me + i], 1)
+    for copy in slot_copies:
+        copy.wait()
+
+    def send_to(j, parts, when):
+        @pl.when(jnp.logical_and(j < me, when))
+        def _():
+            i = j + grp_size - me
+            for h in parts:
+                pltpu.make_async_remote_copy(
+                    src_ref=slots_v.at[h, :, pl.ds(j * cap, cap)],
+                    dst_ref=recv_v.at[h, i - 1],
+                    send_sem=send_sem,
+                    recv_sem=recv_sem.at[h],
+                    device_id=(j, row),
+                    device_id_type=MESH,
+                ).start()
+
+    def send_back(allowed, parts, when):
+        for j in range(grp_size // 4):
+            if allowed(j):
+                send_to(j, parts, when(j))
+        for some in (parts[: len(parts) // 2], parts[len(parts) // 2 :]):
+            for j in range(grp_size // 4, grp_size - 1):
+                if some and allowed(j):
+                    send_to(j, some, when(j))
+
+    every = list(range(PARTS))
+    send_back(lambda j: True, every, lambda j: side >= j % wide)
+
+    def send_one(i, when):
+        @pl.when(
+            jnp.logical_and(
+                jnp.logical_and(when, me + i < grp_size - 1), row < row_size - 1
+            )
+        )
+        def _():
+            for h in range(PARTS // 2):
+                arrivals[h, i].start()
+
+        @pl.when(jnp.logical_and(when, me + i == grp_size - 1))
+        def _():
             for h in range(PARTS):
                 arrivals[h, i].start()
+
+    def send_later(i):
+        above = jnp.logical_and(me + i < grp_size, lax.rem(me + i, wide) >= side)
+
+        @pl.when(above)
+        def _():
+            pl.semaphore_wait(ready_sem.at[me + i], 1)
+
+        if wide == 2 and i % 2 == 0:
+            send_one(i - 1, jnp.logical_and(above, side == 1))
+        send_one(i, above)
+        if i == 1:
+            if wide == 2:
+                send_back(lambda j: j % wide == 1, every, lambda j: side == 0)
+
+            @pl.when(row == 1)
+            def _():
+                pl.semaphore_wait(near_sem.at[1], 1)
+                pl.semaphore_wait(far_sem.at[0], 1)
+                pl.semaphore_signal(
+                    far_sem.at[1], inc=1, device_id=(me, row_size - 1), device_id_type=MESH
+                )
+
+    def tell_left():
+        @pl.when(row == row_size - 1)
+        def _():
+            pl.semaphore_wait(far_sem.at[1], 1)
+            greet(me > 0, near_sem.at[0], (me - 1, row))
+            greet(last, near_sem.at[1], right_id)
+
+    def tell_right():
+        @pl.when(jnp.logical_and(row == row_size - 1, me < grp_size - 1))
+        def _():
+            pl.semaphore_wait(near_sem.at[0], 1)
+            pl.semaphore_signal(
+                near_sem.at[1], inc=1, device_id=right_id, device_id_type=MESH
+            )
+
+    def send_rest():
+        for h in range(PARTS):
+            for i in range(1, grp_size):
+                ok = me + i < grp_size - 1
+                if h < PARTS // 2:
+                    ok = jnp.logical_and(ok, row == row_size - 1)
+                pl.when(ok)(arrivals[h, i].start)
 
     for copy in small_copies:
         copy.wait()
@@ -295,6 +391,7 @@
         x = (gll_v[:, level] * metric[None]).reshape(width, elems)
         return jnp.concatenate(split(x), axis=0)
 
+    send_later(1)
     for k in range(chunks):
         gll_copies[k].wait()
 
@@ -308,15 +405,19 @@
             return carry
 
         lax.fori_loop(0, chunk // 2, remap, 0, unroll=True)
-        if k + 1 < grp_size:
-            send_later(k + 1)
-
-    for i in range(chunks + 1, grp_size):
+        if k + 2 < grp_size:
+            send_later(k + 2)
+        if k == 0:
+            tell_left()
+    tell_right()
+
+    for i in range(chunks + 2, grp_size):
         send_later(i)
+    send_rest()
 
     quarter = lax.broadcasted_iota(jnp.int32, (fields, elems), 1) // HALO
-    hear(jnp.logical_not(last), near_sem.at[0])
-    hear(first, near_sem.at[1])
+    hear(jnp.logical_and(odd, row < row_size - 1), near_sem.at[0])
+    hear(jnp.logical_or(jnp.logical_and(odd, row != 1), row == 0), near_sem.at[1])
     halo_copies = []
     for h in range(PARTS):
         picked = [None] * 4
@@ -488,6 +589,7 @@
             pltpu.SemaphoreType.DMA((PARTS, 2)),
             pltpu.SemaphoreType.REGULAR((grp_size,)),
             pltpu.SemaphoreType.REGULAR((2,)),
+            pltpu.SemaphoreType.REGULAR((2,)),
         ],
         compiler_params=pltpu.CompilerParams(
             collective_id=0, has_side_effects=True, vmem_limit_bytes=32 * 1024 * 1024

time: 19.3 us -> 17.1 us (0.89)
  Pallas kernels: 19.2 us -> 16.9 us
    pallas_call x1, Pallas kernels: 17.7 us -> 15.5 us  [on_device(): pl.pallas_call(functools.partial(exchange_kernel, grp_size, row_size), ou...]
where the time goes in v2:
time: 17.1 us; the launch traced here: 17 us
  Pallas kernels  16.9 us (99%)
    pallas_call x1, Pallas kernels, on_device(): pl.pallas_call(functools.partial(exchange_kernel, grp_size, row_size), ou...  15.5 us
    pallas_call x1, Pallas kernels, on_device(): pl.pallas_call(functools.partial(last_part_kernel, row_size), out_shape=j...  1.47 us

profile of v2, /device:TPU:0, one launch (start us, length us, event | category | flops | bytes accessed | tf_op | source)
XLA Modules:
  0.0 17.0 jit_solution(12097462600979618241)
XLA Ops:
  0.0 0.0 copy-start
  0.0 15.5 %exchange.1 = (f32[8,24,16,128]{3,2,1,0:T(8,128)S(1)}, f32[8,32,128]{2,1,0:T(8,128)S(1)}, f32[2,2,8,128]{3,2,1,0:T(8,128)S(1)}) custom-call(f32[8,32,16,128]{3,2,1,0:T(8,128)} %gll_ref.1, f32[16,128]{1,0:T(8,128)} %metric_ref.1, s32[4,1,128]{2,1,0:T(1,128)} %bitcast.1, f32[32,1024]{1,0:T(8,128)} %rate_ref.1, f32[32,1024]{1,0:T(8,128)} %forcing_ref.1, ...), custom_call_target="tpu_custom_call" | custom-call | tf_op jit(solution)/shard_map/exchange/pallas_call | solution.py:560
  15.5 0.0 copy-done
  15.5 1.5 %last_part.1 = f32[8,32,16,128]{3,2,1,0:T(8,128)} custom-call(f32[8,24,16,128]{3,2,1,0:T(8,128)S(1)} %get-tuple-element.8.done_ref, f32[8,32,128]{2,1,0:T(8,128)S(1)} %get-tuple-element.9.tend_ref, f32[2,2,8,128]{3,2,1,0:T(8,128)S(1)} %get-tuple-element.10.halo_ref, s32[4,128]{1,0:T(4,128)S(1)} %copy-done), custom_call_target="tpu_custom_call" | custom-call | tf_op jit(solution)/shard_map/last_part/pallas_call | solution.py:613
Async XLA Ops:
  0.0 15.5 %copy-start = (s32[4,128]{1,0:T(4,128)S(1)}, s32[4,128]{1,0:T(4,128)}, u32[]{:S(2)}) copy-start(s32[4,128]{1,0:T(4,128)} %neighbours_ref.3) | copy-start | bytes 6148

commit v3 on v2

--- a/solution.py
+++ b/solution.py
@@ -131,6 +131,9 @@
     ready_sem,
     near_sem,
     far_sem,
+    relay_v,
+    relay_send_sem,
+    relay_recv_sem,
 ):
     fields, levels, nodes, elems = gll_v.shape
     part = levels // PARTS
@@ -268,21 +271,61 @@
     every = list(range(PARTS))
     send_back(lambda j: True, every, lambda j: side >= j % wide)
 
+    far_first = row == row_size - 1
+    hop = grp_size // (4 * wide) * wide
+    relays = jnp.logical_and(me >= hop, me < 2 * hop)
+
     def send_one(i, when):
         @pl.when(
             jnp.logical_and(
-                jnp.logical_and(when, me + i < grp_size - 1), row < row_size - 1
+                jnp.logical_and(when, me + i < grp_size), jnp.logical_not(far_first)
             )
         )
         def _():
             for h in range(PARTS // 2):
                 arrivals[h, i].start()
 
-        @pl.when(jnp.logical_and(when, me + i == grp_size - 1))
+        @pl.when(
+            jnp.logical_and(
+                jnp.logical_and(when, me + i == grp_size - 1),
+                jnp.logical_and(far_first, me >= hop),
+            )
+        )
         def _():
             for h in range(PARTS):
                 arrivals[h, i].start()
 
+        if i < grp_size - hop:
+            @pl.when(
+                jnp.logical_and(
+                    jnp.logical_and(when, me + i == grp_size - 1),
+                    jnp.logical_and(far_first, relays),
+                )
+            )
+            def _():
+                for h in range(PARTS):
+                    held = relay_v.at[h]
+                    pltpu.make_async_copy(held, held, relay_recv_sem.at[h]).wait()
+                    pltpu.make_async_remote_copy(
+                        src_ref=held,
+                        dst_ref=recv_v.at[h, i + hop - 1],
+                        send_sem=relay_send_sem,
+                        recv_sem=recv_sem.at[h],
+                        device_id=(grp_size - 1, row),
+                        device_id_type=MESH,
+                    ).start()
+
+    def hand_over():
+        for h in range(PARTS):
+            pltpu.make_async_remote_copy(
+                src_ref=slots_v.at[h, :, block_of(grp_size - 1)],
+                dst_ref=relay_v.at[h],
+                send_sem=send_sem,
+                recv_sem=relay_recv_sem.at[h],
+                device_id=(me + hop, row),
+                device_id_type=MESH,
+            ).start()
+
     def send_later(i):
         above = jnp.logical_and(me + i < grp_size, lax.rem(me + i, wide) >= side)
 
@@ -292,6 +335,8 @@
 
         if wide == 2 and i % 2 == 0:
             send_one(i - 1, jnp.logical_and(above, side == 1))
+        if i == hop:
+            pl.when(jnp.logical_and(far_first, me < hop))(hand_over)
         send_one(i, above)
         if i == 1:
             if wide == 2:
@@ -321,12 +366,20 @@
             )
 
     def send_rest():
-        for h in range(PARTS):
+        for some in (range(PARTS // 2), range(PARTS // 2, PARTS)):
             for i in range(1, grp_size):
                 ok = me + i < grp_size - 1
-                if h < PARTS // 2:
-                    ok = jnp.logical_and(ok, row == row_size - 1)
-                pl.when(ok)(arrivals[h, i].start)
+                if some[0] == 0:
+                    ok = jnp.logical_and(ok, far_first)
+                else:
+                    ok = jnp.logical_or(
+                        ok, jnp.logical_and(me + i == grp_size - 1, jnp.logical_not(far_first))
+                    )
+
+                @pl.when(ok)
+                def _():
+                    for h in some:
+                        arrivals[h, i].start()
 
     for copy in small_copies:
         copy.wait()
@@ -392,6 +445,7 @@
         return jnp.concatenate(split(x), axis=0)
 
     send_later(1)
+    send_later(2)
     for k in range(chunks):
         gll_copies[k].wait()
 
@@ -405,13 +459,13 @@
             return carry
 
         lax.fori_loop(0, chunk // 2, remap, 0, unroll=True)
-        if k + 2 < grp_size:
-            send_later(k + 2)
+        if k + 3 < grp_size:
+            send_later(k + 3)
         if k == 0:
             tell_left()
     tell_right()
 
-    for i in range(chunks + 2, grp_size):
+    for i in range(chunks + 3, grp_size):
         send_later(i)
     send_rest()
 
@@ -478,6 +532,11 @@
             halo_copies.append(copy)
 
     pltpu.make_async_copy(recv_v, recv_v, send_sem).wait()
+
+    @pl.when(jnp.logical_and(far_first, relays))
+    def _():
+        pltpu.make_async_copy(relay_v, relay_v, relay_send_sem).wait()
+
     write = nodes_writer(row_size, neighbours_v[...], fields, elems)
     for h in range(PARTS - 1):
         halo_copies[2 * h].wait()
@@ -495,7 +554,7 @@
                 )
             return carry
 
-        lax.fori_loop(h * packs, (h + 1) * packs, group, 0)
+        lax.fori_loop(h * packs, (h + 1) * packs, group, 0, unroll=True)
     for copy in halo_copies[2 * PARTS - 2 :]:
         copy.wait()
     for way in range(2):
@@ -590,6 +649,9 @@
             pltpu.SemaphoreType.REGULAR((grp_size,)),
             pltpu.SemaphoreType.REGULAR((2,)),
             pltpu.SemaphoreType.REGULAR((2,)),
+            pltpu.VMEM((PARTS, 2 * part, cap), jnp.float32),
+            pltpu.SemaphoreType.DMA,
+            pltpu.SemaphoreType.DMA((PARTS,)),
         ],
         compiler_params=pltpu.CompilerParams(
             collective_id=0, has_side_effects=True, vmem_limit_bytes=32 * 1024 * 1024

time: 17.1 us -> 16.5 us (0.965)
  Pallas kernels: 16.9 us -> 16.3 us
    pallas_call x1, Pallas kernels: 15.5 us -> 14.9 us  [on_device(): pl.pallas_call(functools.partial(exchange_kernel, grp_size, row_size), ou...]
where the time goes in v3:
time: 16.5 us; the launch traced here: 16.4 us
  Pallas kernels  16.3 us (99%)
    pallas_call x1, Pallas kernels, on_device(): pl.pallas_call(functools.partial(exchange_kernel, grp_size, row_size), ou...  14.9 us
    pallas_call x1, Pallas kernels, on_device(): pl.pallas_call(functools.partial(last_part_kernel, row_size), out_shape=j...  1.47 us

profile of v3, /device:TPU:0, one launch (start us, length us, event | category | flops | bytes accessed | tf_op | source)
XLA Modules:
  0.0 16.4 jit_solution(1669890021723060086)
XLA Ops:
  0.0 0.0 copy-start
  0.0 14.9 %exchange.1 = (f32[8,24,16,128]{3,2,1,0:T(8,128)S(1)}, f32[8,32,128]{2,1,0:T(8,128)S(1)}, f32[2,2,8,128]{3,2,1,0:T(8,128)S(1)}) custom-call(f32[8,32,16,128]{3,2,1,0:T(8,128)} %gll_ref.1, f32[16,128]{1,0:T(8,128)} %metric_ref.1, s32[4,1,128]{2,1,0:T(1,128)} %bitcast.1, f32[32,1024]{1,0:T(8,128)} %rate_ref.1, f32[32,1024]{1,0:T(8,128)} %forcing_ref.1, ...), custom_call_target="tpu_custom_call" | custom-call | tf_op jit(solution)/shard_map/exchange/pallas_call | solution.py:619
  14.9 0.0 copy-done
  14.9 1.5 %last_part.1 = f32[8,32,16,128]{3,2,1,0:T(8,128)} custom-call(f32[8,24,16,128]{3,2,1,0:T(8,128)S(1)} %get-tuple-element.8.done_ref, f32[8,32,128]{2,1,0:T(8,128)S(1)} %get-tuple-element.9.tend_ref, f32[2,2,8,128]{3,2,1,0:T(8,128)S(1)} %get-tuple-element.10.halo_ref, s32[4,128]{1,0:T(4,128)S(1)} %copy-done), custom_call_target="tpu_custom_call" | custom-call | tf_op jit(solution)/shard_map/last_part/pallas_call | solution.py:675
Async XLA Ops:
  0.0 14.9 %copy-start = (s32[4,128]{1,0:T(4,128)S(1)}, s32[4,128]{1,0:T(4,128)}, u32[]{:S(2)}) copy-start(s32[4,128]{1,0:T(4,128)} %neighbours_ref.3) | copy-start | bytes 6148

commit v4 on v3

--- a/solution.py
+++ b/solution.py
@@ -282,13 +282,13 @@
             )
         )
         def _():
-            for h in range(PARTS // 2):
+            for h in range(PARTS - 1):
                 arrivals[h, i].start()
 
         @pl.when(
             jnp.logical_and(
                 jnp.logical_and(when, me + i == grp_size - 1),
-                jnp.logical_and(far_first, me >= hop),
+                jnp.logical_and(far_first, me >= 2 * hop),
             )
         )
         def _():
@@ -304,6 +304,7 @@
             )
             def _():
                 for h in range(PARTS):
+                    arrivals[h, i].start()
                     held = relay_v.at[h]
                     pltpu.make_async_copy(held, held, relay_recv_sem.at[h]).wait()
                     pltpu.make_async_remote_copy(
@@ -366,20 +367,19 @@
             )
 
     def send_rest():
-        for some in (range(PARTS // 2), range(PARTS // 2, PARTS)):
-            for i in range(1, grp_size):
-                ok = me + i < grp_size - 1
-                if some[0] == 0:
-                    ok = jnp.logical_and(ok, far_first)
-                else:
-                    ok = jnp.logical_or(
-                        ok, jnp.logical_and(me + i == grp_size - 1, jnp.logical_not(far_first))
-                    )
-
-                @pl.when(ok)
-                def _():
-                    for h in some:
-                        arrivals[h, i].start()
+        for i in range(1, grp_size):
+
+            @pl.when(jnp.logical_and(me + i < grp_size - 1, far_first))
+            def _():
+                for h in range(PARTS - 1):
+                    arrivals[h, i].start()
+
+        for i in range(1, grp_size):
+            ok = jnp.logical_or(
+                me + i < grp_size - 1,
+                jnp.logical_and(me + i == grp_size - 1, jnp.logical_not(far_first)),
+            )
+            pl.when(ok)(arrivals[PARTS - 1, i].start)
 
     for copy in small_copies:
         copy.wait()

time: 16.5 us -> 16.3 us (0.988)
  Pallas kernels: 16.3 us -> 16.1 us
    pallas_call x1, Pallas kernels: 14.9 us -> 14.6 us  [on_device(): pl.pallas_call(functools.partial(exchange_kernel, grp_size, row_size), ou...]
where the time goes in v4:
time: 16.3 us; the launch traced here: 16.1 us
  Pallas kernels  16.1 us (99%)
    pallas_call x1, Pallas kernels, on_device(): pl.pallas_call(functools.partial(exchange_kernel, grp_size, row_size), ou...  14.6 us
    pallas_call x1, Pallas kernels, on_device(): pl.pallas_call(functools.partial(last_part_kernel, row_size), out_shape=j...  1.47 us

profile of v4, /device:TPU:0, one launch (start us, length us, event | category | flops | bytes accessed | tf_op | source)
XLA Modules:
  0.0 16.1 jit_solution(11585810599608760476)
XLA Ops:
  0.0 0.0 copy-start
  0.0 14.6 %exchange.1 = (f32[8,24,16,128]{3,2,1,0:T(8,128)S(1)}, f32[8,32,128]{2,1,0:T(8,128)S(1)}, f32[2,2,8,128]{3,2,1,0:T(8,128)S(1)}) custom-call(f32[8,32,16,128]{3,2,1,0:T(8,128)} %gll_ref.1, f32[16,128]{1,0:T(8,128)} %metric_ref.1, s32[4,1,128]{2,1,0:T(1,128)} %bitcast.1, f32[32,1024]{1,0:T(8,128)} %rate_ref.1, f32[32,1024]{1,0:T(8,128)} %forcing_ref.1, ...), custom_call_target="tpu_custom_call" | custom-call | tf_op jit(solution)/shard_map/exchange/pallas_call | solution.py:619
  14.6 0.0 copy-done
  14.7 1.5 %last_part.1 = f32[8,32,16,128]{3,2,1,0:T(8,128)} custom-call(f32[8,24,16,128]{3,2,1,0:T(8,128)S(1)} %get-tuple-element.8.done_ref, f32[8,32,128]{2,1,0:T(8,128)S(1)} %get-tuple-element.9.tend_ref, f32[2,2,8,128]{3,2,1,0:T(8,128)S(1)} %get-tuple-element.10.halo_ref, s32[4,128]{1,0:T(4,128)S(1)} %copy-done), custom_call_target="tpu_custom_call" | custom-call | tf_op jit(solution)/shard_map/last_part/pallas_call | solution.py:675
Async XLA Ops:
  0.0 14.6 %copy-start = (s32[4,128]{1,0:T(4,128)S(1)}, s32[4,128]{1,0:T(4,128)}, u32[]{:S(2)}) copy-start(s32[4,128]{1,0:T(4,128)} %neighbours_ref.3) | copy-start | bytes 6148
